TPU v7x, 256 devices: a whole 4x4x8 slice. The times are simulated.
256 devices in a mesh: expert: 16 (over x, y), tensor: 8 (over z), replica: 2 (over core).
Axes of the slice: x: 4, y: 4, z: 8, core: 2. Of those that a mesh axis runs over, the one named last changes fastest.
Arguments:
- trained: float32 [16, 7168, 2048], P('replica', 'tensor', 'expert'), may hold values from -3080 to 3080
- snapshot: bfloat16 [16, 7168, 2048], P('replica', 'tensor', 'expert'), may hold values from -3072 to 3072
- changed: int32 [16, 56, 16], P('replica', 'tensor', 'expert'), may hold values from 0 to 1, as said below
- placement: int32 [16], replicated, may hold values from 0 to 15, each once
Outputs:
- rotated_update: bfloat16 [16, 7168, 2048], P('expert', None, 'tensor')
Inputs may be any that keep to these rules, and one draw needn't show every extreme that they name: `placement`: each of the 16 experts appears exactly once. `changed`: in each aligned block of 7 block rows by 1 block columns of one expert, at most 4 entries are 1; for every expert some such block has exactly 4.
All inputs are finite; a program needn't handle non-finite values.
Results may differ from a plain program's by a relative error of at most 0.001.
Values may be sent and summed in bfloat16 or wider, within the bound.
A program may use at most 64 MiB of HBM per device.

v0:
```python
import math
import jax
import jax.numpy as jnp
from jax import lax
from jax.sharding import PartitionSpec as P

BLK = 128


def hadamard():
    positions = jnp.arange(BLK, dtype=jnp.int32)
    parity = jnp.zeros((BLK, BLK), jnp.int32)
    for bit_level in range(BLK.bit_length() - 1):
        parity = parity + (positions[:, None] >> bit_level & 1) * (
            positions[None, :] >> bit_level & 1
        )
    return (1 - 2 * (parity % 2)).astype(jnp.float32) / math.sqrt(BLK)


def body(trained, snapshot, changed, placement):
    hadamard_table = hadamard()
    local_experts, local_rows, local_cols = trained.shape
    copies = lax.axis_size("replica")
    tensor_count = lax.axis_size("tensor")
    expert_count = lax.axis_size("expert")
    members = expert_count // tensor_count
    slot_total = placement.shape[0]
    owner_slots = slot_total // expert_count
    block_rows = local_rows // BLK
    block_cols = local_cols // BLK
    part_rows = BLK // copies
    block_count = block_rows * block_cols
    capacity = (4 * block_count + 3) // 7
    block_flags = changed.reshape(local_experts, block_count)
    position = jnp.arange(block_count, dtype=jnp.int32)
    ranking = jnp.where(block_flags == 1, position[None, :], block_count + position[None, :])
    picked = jnp.argsort(ranking, axis=1)[:, :capacity]
    used_slots = jnp.take_along_axis(block_flags, picked, axis=1)
    expert_ids = jnp.arange(local_experts, dtype=jnp.int32)[:, None]
    row_ids = picked // block_cols
    col_ids = picked % block_cols
    new_tiles = trained.reshape(local_experts, block_rows, BLK, block_cols, BLK)[
        expert_ids, row_ids, :, col_ids, :
    ]
    old_tiles = snapshot.reshape(local_experts, block_rows, BLK, block_cols, BLK)[
        expert_ids, row_ids, :, col_ids, :
    ]
    delta_tiles = jnp.where(
        used_slots[:, :, None, None] == 1, new_tiles - old_tiles.astype(jnp.float32), 0.0
    )
    coded_tiles = jnp.einsum(
        "ij,pmjk->pmik", hadamard_table, delta_tiles, precision=lax.Precision.HIGHEST
    ).astype(jnp.bfloat16)
    coded_tiles = coded_tiles.reshape(local_experts, capacity, copies, part_rows, BLK)
    spots_pair = jnp.broadcast_to(picked[:, :, None], (local_experts, capacity, copies))
    tiles_all, spots_all = (
        lax.all_to_all(coded_tiles, "replica", split_axis=2, concat_axis=0, tiled=True),
        lax.all_to_all(spots_pair, "replica", split_axis=2, concat_axis=0, tiled=True),
    )
    chosen = jnp.take(tiles_all, placement, axis=0).reshape(
        slot_total, 1, 1, capacity, part_rows, BLK
    )
    chosen_spots = jnp.take(spots_all, placement, axis=0).reshape(slot_total, 1, 1, capacity)
    tiles_in, spot_numbers = (
        lax.all_to_all(
            lax.all_to_all(chosen, "expert", split_axis=0, concat_axis=2, tiled=True),
            "tensor",
            split_axis=2,
            concat_axis=1,
            tiled=True,
        ),
        lax.all_to_all(
            lax.all_to_all(chosen_spots, "expert", split_axis=0, concat_axis=2, tiled=True),
            "tensor",
            split_axis=2,
            concat_axis=1,
            tiled=True,
        ),
    )
    source_count = tiles_in.shape[1]
    one_hot = (spot_numbers[..., None] == position).astype(jnp.bfloat16)
    placed = jnp.einsum(
        "osnmg,osnmab->osngab", one_hot, tiles_in, preferred_element_type=jnp.float32
    ).astype(jnp.bfloat16)
    placed = placed.reshape(
        owner_slots, source_count, members, block_rows, block_cols, part_rows, BLK
    )
    placed = jnp.transpose(placed, (0, 1, 3, 5, 2, 4, 6))
    owner_cols = members * block_cols * BLK
    owned_rows = placed.reshape(owner_slots, source_count, block_rows, 1, part_rows, owner_cols)
    whole_rows = lax.all_gather(owned_rows, "replica", axis=3, tiled=True)
    return whole_rows.reshape(owner_slots, tensor_count * block_rows * BLK, owner_cols)


def solution(mesh):
    in_specs = (
        P("replica", "tensor", "expert"),
        P("replica", "tensor", "expert"),
        P("replica", "tensor", "expert"),
        P(),
    )
    out_specs = P("expert", None, "tensor")
    return jax.shard_map(body, mesh=mesh, in_specs=in_specs, out_specs=out_specs, check_vma=False)
```

profile of v0, /device:TPU:1, one launch (start us, length us, event | category | flops | bytes accessed | tf_op | source)
XLA Modules:
  0.0 145.1 jit_solution(11660733728816668597)
XLA Ops:
  6.5 0.0 copy-start
  6.5 0.9 iota_select_fusion
  7.4 0.7 sort.17
  8.1 0.6 broadcast_in_dim.55
  8.7 6.4 %all-to-all-start = ((s32[8,4,2]{0,1,2:T(4,128)}), s32[8,4,2]{0,1,2:T(4,128)S(1)}, u32[]{:S(2)}, u32[]{:S(2)}) async-start(s32[8,4,2]{0,1,2:T(4,128)} %broadcast_in_dim.55), calls=%async_computation | async-start | bytes 8192 | tf_op jit(solution)/shard_map/all_to_all | solution.py:58
  15.1 0.7 compare_and_fusion
  15.8 0.7 compare_select_fusion.1
  16.4 0.8 copy.38
  17.2 0.1 copy.46
  17.3 0.1 reshape.261
  17.4 0.7 gather_fusion.4
  18.1 0.1 reshape.264
  18.1 0.1 copy.47
  18.2 0.1 copy.48
  18.3 0.0 copy-done
  18.3 0.8 gather_fusion.2
  19.1 4.0 %gather_fusion.1 = f32[32,128,128]{2,1,0:T(8,128)} fusion(f32[8,7,128,1,128]{4,2,1,0,3:T(8,128)} %bitcast.67, s32[32]{0:T(128)S(1)} %reshape.261), kind=kCustom, calls=%fused_computation.1 | custom fusion | bytes 4194688 | tf_op jit(solution)/shard_map/gather | solution.py:42
  23.2 1.9 %convert_subtract_fusion = f32[32,128,128]{2,1,0:T(8,128)S(1)} fusion(f32[32,128,128]{2,1,0:T(8,128)} %gather_fusion.1, bf16[32,128,128]{2,1,0:T(8,128)(2,1)S(1)} %gather_fusion.2), kind=kLoop, calls=%fused_computation.5 | loop fusion | flops 1048576 | bytes 5242880 | tf_op jit(solution)/shard_map/sub | solution.py:49
  25.0 2.3 %fusion.2 = bf16[8,4,128,128]{2,3,1,0:T(8,128)(2,1)S(1)} fusion(f32[8,4,128,128]{3,2,1,0:T(8,128)S(1)} %bitcast.61, pred[8,4]{1,0:T(8,128)(4,1)S(1)} %copy.48, s32[128]{0:T(128)S(1)} %get-tuple-element.7, s32[128]{0:T(128)S(1)} %get-tuple-element.8, s32[128]{0:T(128)S(1)} %get-tuple-element.9, s32[128]{0:T(128)S(1)} %get-tuple-element.10, ...), kind=kOutput, calls=%fused_computation.9 | convolution fusion | flops 806813696 | bytes 3149344 | tf_op jit(solution)/shard_map/ij,pmjk->pmik/dot_general | solution.py:51
  27.3 1.1 copy.49
  28.4 0.0 all-to-all-done
  28.4 3.6 %all-to-all-start.3 = ((bf16[8,4,2,64,128]{4,3,1,0,2:T(8,128)(2,1)}), bf16[8,4,2,64,128]{4,3,1,0,2:T(8,128)(2,1)S(1)}, u32[]{:S(2)}, u32[]{:S(2)}) async-start(bf16[8,4,2,64,128]{4,3,1,0,2:T(8,128)(2,1)} %copy.49), calls=%async_computation.3 | async-start | bytes 2097152 | tf_op jit(solution)/shard_map/all_to_all | solution.py:57
  32.0 0.1 copy.59
  32.1 0.6 gather_fusion
  32.6 0.1 copy.42
  32.7 0.7 copy.43
  33.4 0.3 all-to-all-done.3
  33.7 0.0 copy-start.1
  33.7 5.1 %all-to-all-start.1 = ((s32[16,1,1,4]{3,2,1,0:T(1,128)}), s32[16,1,1,4]{3,2,1,0:T(1,128)}, u32[]{:S(2)}, u32[]{:S(2)}) async-start(s32[16,1,1,4]{3,2,1,0:T(1,128)} %copy.43), calls=%async_computation.1 | async-start | bytes 16384 | tf_op jit(solution)/shard_map/all_to_all | solution.py:73
  38.9 0.0 copy-done.1
  38.9 2.0 %gather_fusion.3 = bf16[16,4,64,128]{3,2,1,0:T(8,128)(2,1)S(1)} fusion(bf16[16,4,64,128]{3,2,1,0:T(8,128)(2,1)} %bitcast.65, s32[1024]{0:T(1024)S(1)} %pad_clamp_fusion), kind=kCustom, calls=%fused_computation.3 | custom fusion | bytes 2097216 | tf_op jit(solution)/shard_map/jit(_take)/gather | solution.py:60
  40.8 1.1 fusion.5
  42.0 3.2 %all-to-all-done.1 = s32[16,1,1,4]{3,2,1,0:T(1,128)} async-done(((s32[16,1,1,4]{3,2,1,0:T(1,128)}), s32[16,1,1,4]{3,2,1,0:T(1,128)}, u32[]{:S(2)}, u32[]{:S(2)}) %all-to-all-start.1) | async-done | bytes 288 | tf_op jit(solution)/shard_map/all_to_all | solution.py:73
  45.2 18.6 %all_to_all.78 = bf16[16,1,1,4,64,128]{5,4,3,2,1,0:T(8,128)(2,1)S(1)} all-to-all(bf16[16,1,1,4,64,128]{5,4,3,2,1,0:T(8,128)(2,1)} %fusion.5), channel_id=1, replica_groups=mesh['expert'=16,'tensor'=8,'replica'=2] {'expert'}, dimensions={0} | all-to-all | bytes 2097152 | tf_op jit(solution)/shard_map/all_to_all | solution.py:66
  63.8 32.6 %all_to_all.79 = bf16[1,1,16,4,64,128]{5,4,3,1,0,2:T(8,128)(2,1)} all-to-all(bf16[1,1,16,4,64,128]{5,4,3,1,0,2:T(8,128)(2,1)S(1)} %bitcast.66), channel_id=1, replica_groups=mesh['expert'=16,'tensor'=8,'replica'=2] {'tensor'}, dimensions={2} | all-to-all | bytes 2097152 | tf_op jit(solution)/shard_map/all_to_all | solution.py:65
  96.3 4.3 %all-to-all-start.2 = ((s32[1,1,16,4]{3,1,0,2:T(1,128)}), s32[1,1,16,4]{3,1,0,2:T(1,128)S(1)}, u32[]{:S(2)}, u32[]{:S(2)}) async-start(s32[1,1,16,4]{3,1,0,2:T(1,128)} %bitcast.31), calls=%async_computation.2 | async-start | bytes 16384 | tf_op jit(solution)/shard_map/all_to_all | solution.py:72
  100.6 0.0 all-gather.2.cloned.1.call-start
  100.7 2.1 %copy.52 = bf16[1,1,16,4,64,128]{5,3,4,2,1,0:T(4,128)(2,1)S(1)} copy(bf16[1,1,16,4,64,128]{5,4,3,1,0,2:T(8,128)(2,1)} %all_to_all.79) | data formatting | bytes 2097152 | tf_op jit(solution)/shard_map/all_to_all | solution.py:65
  102.8 4.4 %all-to-all-done.2 = s32[1,1,16,4]{3,1,0,2:T(1,128)S(1)} async-done(((s32[1,1,16,4]{3,1,0,2:T(1,128)}), s32[1,1,16,4]{3,1,0,2:T(1,128)S(1)}, u32[]{:S(2)}, u32[]{:S(2)}) %all-to-all-start.2) | async-done | bytes 288 | tf_op jit(solution)/shard_map/all_to_all | solution.py:72
  107.2 1.3 convert_bitcast_fusion
  108.5 3.3 %copy.53 = bf16[1,8,7,64,2,1,128]{6,4,3,2,1,5,0:T(2,128)(2,1)} copy(bf16[1,8,7,64,2,1,128]{6,2,3,4,1,5,0:T(8,128)(2,1)S(1)} %convert_bitcast_fusion) | data formatting | bytes 3670016 | tf_op jit(solution)/shard_map/transpose | solution.py:88
  111.8 5.3 %reshape.227 = bf16[1,8,7,1,64,256]{5,4,2,1,3,0:T(8,128)(2,1)} reshape(bf16[1,8,7,64,2,1,128]{6,4,3,2,1,5,0:T(2,128)(2,1)} %copy.53) | data formatting | bytes 3670016 | tf_op jit(solution)/shard_map/reshape | solution.py:90
  117.1 0.0 all-gather.2.cloned.1.call-update
  117.1 16.8 %all-gather.2.cloned.1.call-done = bf16[1,8,7,2,64,256]{5,4,2,1,0,3:T(8,128)(2,1)} async-done(((bf16[1,8,7,1,64,256]{5,4,2,1,0,3:T(8,128)(2,1)}), bf16[1,8,7,2,64,256]{5,4,2,1,0,3:T(8,128)(2,1)}) %all-gather.2.cloned.1.call-update) | async-done | bytes 3670032 | tf_op jit(solution)/shard_map/all_gather | solution.py:91
  133.9 4.4 %copy.55 = bf16[1,8,7,2,64,256]{5,4,3,2,1,0:T(8,128)(2,1)} copy(bf16[1,8,7,2,64,256]{5,4,2,1,0,3:T(8,128)(2,1)} %all-gather.2.cloned.1.call-done) | data formatting | bytes 7340032 | tf_op jit(solution)/shard_map/all_gather | solution.py:91
  (11 shorter events, 0.1 us)
Async XLA Ops:
  6.5 11.8 %copy-start = (bf16[8,896,128]{2,1,0:T(8,128)(2,1)S(1)}, bf16[8,896,128]{2,1,0:T(8,128)(2,1)}, u32[]{:S(2)}) copy-start(bf16[8,896,128]{2,1,0:T(8,128)(2,1)} %param.5) | copy-start | bytes 5505028
  8.7 19.7 %all-to-all-start = ((s32[8,4,2]{0,1,2:T(4,128)}), s32[8,4,2]{0,1,2:T(4,128)S(1)}, u32[]{:S(2)}, u32[]{:S(2)}) async-start(s32[8,4,2]{0,1,2:T(4,128)} %broadcast_in_dim.55), calls=%async_computation | async-start | bytes 8192 | tf_op jit(solution)/shard_map/all_to_all | solution.py:58
  28.4 5.3 %all-to-all-start.3 = ((bf16[8,4,2,64,128]{4,3,1,0,2:T(8,128)(2,1)}), bf16[8,4,2,64,128]{4,3,1,0,2:T(8,128)(2,1)S(1)}, u32[]{:S(2)}, u32[]{:S(2)}) async-start(bf16[8,4,2,64,128]{4,3,1,0,2:T(8,128)(2,1)} %copy.49), calls=%async_computation.3 | async-start | bytes 2097152 | tf_op jit(solution)/shard_map/all_to_all | solution.py:57
  33.7 5.1 %copy-start.1 = (bf16[8,4,2,64,128]{4,3,1,0,2:T(8,128)(2,1)}, bf16[8,4,2,64,128]{4,3,1,0,2:T(8,128)(2,1)S(1)}, u32[]{:S(2)}) copy-start(bf16[8,4,2,64,128]{4,3,1,0,2:T(8,128)(2,1)S(1)} %all-to-all-done.3) | copy-start | bytes 3145732
  33.7 11.4 %all-to-all-start.1 = ((s32[16,1,1,4]{3,2,1,0:T(1,128)}), s32[16,1,1,4]{3,2,1,0:T(1,128)}, u32[]{:S(2)}, u32[]{:S(2)}) async-start(s32[16,1,1,4]{3,2,1,0:T(1,128)} %copy.43), calls=%async_computation.1 | async-start | bytes 16384 | tf_op jit(solution)/shard_map/all_to_all | solution.py:73
  96.3 10.8 %all-to-all-start.2 = ((s32[1,1,16,4]{3,1,0,2:T(1,128)}), s32[1,1,16,4]{3,1,0,2:T(1,128)S(1)}, u32[]{:S(2)}, u32[]{:S(2)}) async-start(s32[1,1,16,4]{3,1,0,2:T(1,128)} %bitcast.31), calls=%async_computation.2 | async-start | bytes 16384 | tf_op jit(solution)/shard_map/all_to_all | solution.py:72
  100.6 33.3 %all-gather.2.cloned.1.call-start = ((), (), s32[]{:S(2)}) async-start(), calls=%async_computation.6 | async-start | bytes 5505024 | tf_op jit(solution)/shard_map/all_gather | solution.py:91
Sparse Core Ops, SparseCore 0:
  117.2 16.6 all-gather.1
where the time goes:
time: 146 us; the launch traced here: 145 us
  blocking collectives  51.2 us (35%)
  local copies, waits for them, and re-layouts  26.8 us (18%)
  waiting for transfers between devices  24.8 us (17%)
  starting transfers between devices  19.4 us (13%)
  between operations  13.5 us (9%)
  other arithmetic  5.93 us (4%)
  matrix products  3.58 us (2%)
    all_to_all x1, blocking collectives, body(): lax.all_to_all(lax.all_to_all(chosen, 'expert', split_axis=0, concat_axis...  32.6 us
    all_to_all x1, blocking collectives, body(): lax.all_to_all(chosen, 'expert', split_axis=0, concat_axis=2, tiled=True)  18.6 us
    all_gather x1, waiting for transfers between devices, body(): whole_rows = lax.all_gather(owned_rows, 'replica', axis=3, tiled=True)  16.8 us
    all_to_all x1, starting transfers between devices, body(): lax.all_to_all(spots_pair, 'replica', split_axis=2, concat_axis=0, tiled=...  6.41 us
    reshape x1, local copies, waits for them, and re-layouts, body(): placed.reshape(owner_slots, source_count, block_rows, 1, part_rows, owner...  5.3 us
    all_to_all x1, starting transfers between devices, body(): lax.all_to_all(chosen_spots, 'expert', split_axis=0, concat_axis=2, tiled...  5.1 us
    all_to_all x1, waiting for transfers between devices, body(): lax.all_to_all(lax.all_to_all(chosen_spots, 'expert', split_axis=0, conca...  4.42 us
    all_gather x1, local copies, waits for them, and re-layouts, body(): whole_rows = lax.all_gather(owned_rows, 'replica', axis=3, tiled=True)  4.37 us
  transfers between devices with their start and end apart: 5, of which 4 were waited for; matrix products, arithmetic and copies ran while one was open for 14% of the time, Pallas kernels for 0%

commit v1 on v0

--- a/solution.py
+++ b/solution.py
@@ -88,7 +88,8 @@
     placed = jnp.transpose(placed, (0, 1, 3, 5, 2, 4, 6))
     owner_cols = members * block_cols * BLK
     owned_rows = placed.reshape(owner_slots, source_count, block_rows, 1, part_rows, owner_cols)
-    whole_rows = lax.all_gather(owned_rows, "replica", axis=3, tiled=True)
+    copies_2 = jnp.concatenate([owned_rows] * lax.axis_size("replica"), axis=3)
+    whole_rows = lax.all_to_all(copies_2, "replica", 3, 3, tiled=True)
     return whole_rows.reshape(owner_slots, tensor_count * block_rows * BLK, owner_cols)
 
 

time: 146 us -> 127 us (0.87)
  waiting for transfers between devices: 24.8 us -> 8.17 us
  between operations: 13.5 us -> 0.1 us
  blocking collectives: 51.2 us -> 63.1 us
  other arithmetic: 5.93 us -> 8.31 us
  local copies, waits for them, and re-layouts: 26.8 us -> 24.7 us
    all_gather x1 -> x0, waiting for transfers between devices: 16.8 us -> none  [body(): whole_rows = lax.all_gather(owned_rows, 'replica', axis=3, tiled=True)]
    all_to_all x0 -> x1, blocking collectives: none -> 12.4 us  [body(): whole_rows = lax.all_to_all(copies_2, 'replica', 3, 3, tiled=True)]
    all_gather x1 -> x0, local copies, waits for them, and re-layouts: 4.37 us -> none  [body(): whole_rows = lax.all_gather(owned_rows, 'replica', axis=3, tiled=True)]
    concatenate x0 -> x1, other arithmetic: none -> 2.39 us  [body(): copies_2 = jnp.concatenate([owned_rows] * lax.axis_size('replica'), axis=3)]
    all_to_all x0 -> x1, local copies, waits for them, and re-layouts: none -> 2.29 us  [body(): whole_rows = lax.all_to_all(copies_2, 'replica', 3, 3, tiled=True)]
  transfers between devices with their start and end apart: 5 -> 4, of which waited for: 4 -> 3; matrix products, arithmetic and copies ran while one was open for 14% -> 16% of each run, Pallas kernels for 0% -> 0%
where the time goes in v1:
time: 127 us
  blocking collectives  63.1 us (50%)
  local copies, waits for them, and re-layouts  24.7 us (19%)
  starting transfers between devices  18.8 us (15%)
  other arithmetic  8.31 us (7%)
  waiting for transfers between devices  8.17 us (6%)
  matrix products  3.58 us (3%)
    all_to_all x1, blocking collectives, body(): lax.all_to_all(lax.all_to_all(chosen, 'expert', split_axis=0, concat_axis...  32.4 us
    all_to_all x1, blocking collectives, body(): lax.all_to_all(chosen, 'expert', split_axis=0, concat_axis=2, tiled=True)  18.3 us
    all_to_all x1, blocking collectives, body(): whole_rows = lax.all_to_all(copies_2, 'replica', 3, 3, tiled=True)  12.4 us
    all_to_all x1, starting transfers between devices, body(): lax.all_to_all(spots_pair, 'replica', split_axis=2, concat_axis=0, tiled=...  6.41 us
    reshape x1, local copies, waits for them, and re-layouts, body(): placed.reshape(owner_slots, source_count, block_rows, 1, part_rows, owner...  5.27 us
    all_to_all x1, starting transfers between devices, body(): lax.all_to_all(chosen_spots, 'expert', split_axis=0, concat_axis=2, tiled...  5.1 us
    all_to_all x1, waiting for transfers between devices, body(): lax.all_to_all(lax.all_to_all(chosen_spots, 'expert', split_axis=0, conca...  4.47 us
    gather x1, local copies, waits for them, and re-layouts, body(): trained.reshape(local_experts, block_rows, BLK, block_cols, BLK)  4.04 us
  transfers between devices with their start and end apart: 4, of which 3 were waited for; matrix products, arithmetic and copies ran while one was open for 16% of the time, Pallas kernels for 0%

profile of v1, /device:TPU:1, one launch (start us, length us, event | category | flops | bytes accessed | tf_op | source)
XLA Modules:
  0.0 126.7 jit_solution(16195161585949996241)
XLA Ops:
  0.0 0.0 copy-start
  0.0 0.9 iota_select_fusion
  0.9 0.7 sort.17
  1.6 0.6 broadcast_in_dim.55
  2.2 6.4 %all-to-all-start = ((s32[8,4,2]{0,1,2:T(4,128)}), s32[8,4,2]{0,1,2:T(4,128)S(1)}, u32[]{:S(2)}, u32[]{:S(2)}) async-start(s32[8,4,2]{0,1,2:T(4,128)} %broadcast_in_dim.55), calls=%async_computation | async-start | bytes 8192 | tf_op jit(solution)/shard_map/all_to_all | solution.py:58
  8.6 0.7 compare_and_fusion
  9.2 0.7 compare_select_fusion.1
  9.9 0.8 copy.38
  10.7 0.1 copy.46
  10.8 0.1 reshape.261
  10.9 0.7 gather_fusion.4
  11.5 0.1 reshape.264
  11.6 0.1 copy.47
  11.7 0.1 copy.48
  11.8 0.0 copy-done
  11.8 0.8 gather_fusion.2
  12.6 4.0 %gather_fusion.1 = f32[32,128,128]{2,1,0:T(8,128)} fusion(f32[8,7,128,1,128]{4,2,1,0,3:T(8,128)} %bitcast.67, s32[32]{0:T(128)S(1)} %reshape.261), kind=kCustom, calls=%fused_computation.1 | custom fusion | bytes 4194688 | tf_op jit(solution)/shard_map/gather | solution.py:42
  16.6 1.9 %convert_subtract_fusion = f32[32,128,128]{2,1,0:T(8,128)S(1)} fusion(f32[32,128,128]{2,1,0:T(8,128)} %gather_fusion.1, bf16[32,128,128]{2,1,0:T(8,128)(2,1)S(1)} %gather_fusion.2), kind=kLoop, calls=%fused_computation.6 | loop fusion | flops 1048576 | bytes 5242880 | tf_op jit(solution)/shard_map/sub | solution.py:49
  18.5 2.3 %fusion.2 = bf16[8,4,128,128]{2,3,1,0:T(8,128)(2,1)S(1)} fusion(f32[8,4,128,128]{3,2,1,0:T(8,128)S(1)} %bitcast.62, pred[8,4]{1,0:T(8,128)(4,1)S(1)} %copy.48, s32[128]{0:T(128)S(1)} %get-tuple-element.7, s32[128]{0:T(128)S(1)} %get-tuple-element.8, s32[128]{0:T(128)S(1)} %get-tuple-element.9, s32[128]{0:T(128)S(1)} %get-tuple-element.10, ...), kind=kOutput, calls=%fused_computation.10 | convolution fusion | flops 806813696 | bytes 3149344 | tf_op jit(solution)/shard_map/ij,pmjk->pmik/dot_general | solution.py:51
  20.8 1.1 copy.49
  21.9 0.0 all-to-all-done
  21.9 3.6 %all-to-all-start.3 = ((bf16[8,4,2,64,128]{4,3,1,0,2:T(8,128)(2,1)}), bf16[8,4,2,64,128]{4,3,1,0,2:T(8,128)(2,1)S(1)}, u32[]{:S(2)}, u32[]{:S(2)}) async-start(bf16[8,4,2,64,128]{4,3,1,0,2:T(8,128)(2,1)} %copy.49), calls=%async_computation.3 | async-start | bytes 2097152 | tf_op jit(solution)/shard_map/all_to_all | solution.py:57
  25.5 0.1 copy.59
  25.5 0.6 gather_fusion
  26.1 0.1 copy.42
  26.2 0.7 copy.43
  26.9 0.3 all-to-all-done.3
  27.2 0.0 copy-start.1
  27.2 5.1 %all-to-all-start.1 = ((s32[16,1,1,4]{3,2,1,0:T(1,128)}), s32[16,1,1,4]{3,2,1,0:T(1,128)}, u32[]{:S(2)}, u32[]{:S(2)}) async-start(s32[16,1,1,4]{3,2,1,0:T(1,128)} %copy.43), calls=%async_computation.1 | async-start | bytes 16384 | tf_op jit(solution)/shard_map/all_to_all | solution.py:73
  32.3 0.0 copy-done.1
  32.3 2.0 %gather_fusion.3 = bf16[16,4,64,128]{3,2,1,0:T(8,128)(2,1)S(1)} fusion(bf16[16,4,64,128]{3,2,1,0:T(8,128)(2,1)} %bitcast.65, s32[1024]{0:T(1024)S(1)} %pad_clamp_fusion), kind=kCustom, calls=%fused_computation.3 | custom fusion | bytes 2097216 | tf_op jit(solution)/shard_map/jit(_take)/gather | solution.py:60
  34.3 1.1 fusion.5
  35.4 3.4 %all-to-all-done.1 = s32[16,1,1,4]{3,2,1,0:T(1,128)} async-done(((s32[16,1,1,4]{3,2,1,0:T(1,128)}), s32[16,1,1,4]{3,2,1,0:T(1,128)}, u32[]{:S(2)}, u32[]{:S(2)}) %all-to-all-start.1) | async-done | bytes 288 | tf_op jit(solution)/shard_map/all_to_all | solution.py:73
  38.8 18.3 %all_to_all.83 = bf16[16,1,1,4,64,128]{5,4,3,2,1,0:T(8,128)(2,1)S(1)} all-to-all(bf16[16,1,1,4,64,128]{5,4,3,2,1,0:T(8,128)(2,1)} %fusion.5), channel_id=1, replica_groups=mesh['expert'=16,'tensor'=8,'replica'=2] {'expert'}, dimensions={0} | all-to-all | bytes 2097152 | tf_op jit(solution)/shard_map/all_to_all | solution.py:66
  57.1 32.4 %all_to_all.84 = bf16[1,1,16,4,64,128]{5,4,3,1,0,2:T(8,128)(2,1)} all-to-all(bf16[1,1,16,4,64,128]{5,4,3,1,0,2:T(8,128)(2,1)S(1)} %bitcast.66), channel_id=1, replica_groups=mesh['expert'=16,'tensor'=8,'replica'=2] {'tensor'}, dimensions={2} | all-to-all | bytes 2097152 | tf_op jit(solution)/shard_map/all_to_all | solution.py:65
  89.6 3.7 %all-to-all-start.2 = ((s32[1,1,16,4]{3,1,0,2:T(1,128)}), s32[1,1,16,4]{3,1,0,2:T(1,128)S(1)}, u32[]{:S(2)}, u32[]{:S(2)}) async-start(s32[1,1,16,4]{3,1,0,2:T(1,128)} %bitcast.31), calls=%async_computation.2 | async-start | bytes 16384 | tf_op jit(solution)/shard_map/all_to_all | solution.py:72
  93.3 2.1 %copy.52 = bf16[1,1,16,4,64,128]{5,3,4,2,1,0:T(4,128)(2,1)S(1)} copy(bf16[1,1,16,4,64,128]{5,4,3,1,0,2:T(8,128)(2,1)} %all_to_all.84) | data formatting | bytes 2097152 | tf_op jit(solution)/shard_map/all_to_all | solution.py:65
  95.4 4.5 %all-to-all-done.2 = s32[1,1,16,4]{3,1,0,2:T(1,128)S(1)} async-done(((s32[1,1,16,4]{3,1,0,2:T(1,128)}), s32[1,1,16,4]{3,1,0,2:T(1,128)S(1)}, u32[]{:S(2)}, u32[]{:S(2)}) %all-to-all-start.2) | async-done | bytes 288 | tf_op jit(solution)/shard_map/all_to_all | solution.py:72
  99.8 1.3 %convert_bitcast_fusion = bf16[1,8,7,64,2,1,128]{6,2,3,4,1,5,0:T(8,128)(2,1)S(1)} fusion(bf16[8,2,4,64,128]{4,2,3,1,0:T(4,128)(2,1)S(1)} %bitcast.64, s32[8,2,4]{2,1,0:T(2,128)S(1)} %bitcast.69), kind=kOutput, calls=%fused_computation.7 | convolution fusion | flops 8257984 | bytes 2883840 | tf_op jit(solution)/shard_map/osnmg,osnmab->osngab/dot_general | solution.py:82
  101.2 3.3 %copy.53 = bf16[1,8,7,64,2,1,128]{6,4,3,2,1,5,0:T(2,128)(2,1)} copy(bf16[1,8,7,64,2,1,128]{6,2,3,4,1,5,0:T(8,128)(2,1)S(1)} %convert_bitcast_fusion) | data formatting | bytes 3670016 | tf_op jit(solution)/shard_map/transpose | solution.py:88
  104.4 5.3 %reshape.227 = bf16[1,8,7,1,64,256]{5,4,2,1,3,0:T(8,128)(2,1)} reshape(bf16[1,8,7,64,2,1,128]{6,4,3,2,1,5,0:T(2,128)(2,1)} %copy.53) | data formatting | bytes 3670016 | tf_op jit(solution)/shard_map/reshape | solution.py:90
  109.7 2.4 %maximum_bitcast_fusion = bf16[1,8,7,2,64,256]{5,4,2,1,0,3:T(8,128)(2,1)S(1)} fusion(bf16[1,8,7,1,64,256]{5,4,2,1,3,0:T(8,128)(2,1)} %reshape.227), kind=kLoop, calls=%fused_computation.5 | loop fusion | flops 1835008 | bytes 5505024 | tf_op jit(solution)/shard_map/concatenate | solution.py:91
  112.1 12.4 %all_to_all.85 = bf16[1,8,7,2,64,256]{5,4,2,1,0,3:T(8,128)(2,1)S(1)} all-to-all(bf16[1,8,7,2,64,256]{5,4,2,1,0,3:T(8,128)(2,1)S(1)} %maximum_bitcast_fusion), channel_id=1, replica_groups=mesh['expert'=16,'tensor'=8,'replica'=2] {'replica'}, dimensions={3} | all-to-all | bytes 7340032 | tf_op jit(solution)/shard_map/all_to_all | solution.py:92
  124.5 2.3 %copy.55 = bf16[1,8,7,2,64,256]{5,4,3,2,1,0:T(8,128)(2,1)} copy(bf16[1,8,7,2,64,256]{5,4,2,1,0,3:T(8,128)(2,1)S(1)} %all_to_all.85) | data formatting | bytes 7340032 | tf_op jit(solution)/shard_map/all_to_all | solution.py:92
  (11 shorter events, 0.1 us)
Async XLA Ops:
  0.0 11.8 %copy-start = (bf16[8,896,128]{2,1,0:T(8,128)(2,1)S(1)}, bf16[8,896,128]{2,1,0:T(8,128)(2,1)}, u32[]{:S(2)}) copy-start(bf16[8,896,128]{2,1,0:T(8,128)(2,1)} %param.5) | copy-start | bytes 5505028
  2.2 19.7 %all-to-all-start = ((s32[8,4,2]{0,1,2:T(4,128)}), s32[8,4,2]{0,1,2:T(4,128)S(1)}, u32[]{:S(2)}, u32[]{:S(2)}) async-start(s32[8,4,2]{0,1,2:T(4,128)} %broadcast_in_dim.55), calls=%async_computation | async-start | bytes 8192 | tf_op jit(solution)/shard_map/all_to_all | solution.py:58
  21.9 5.3 %all-to-all-start.3 = ((bf16[8,4,2,64,128]{4,3,1,0,2:T(8,128)(2,1)}), bf16[8,4,2,64,128]{4,3,1,0,2:T(8,128)(2,1)S(1)}, u32[]{:S(2)}, u32[]{:S(2)}) async-start(bf16[8,4,2,64,128]{4,3,1,0,2:T(8,128)(2,1)} %copy.49), calls=%async_computation.3 | async-start | bytes 2097152 | tf_op jit(solution)/shard_map/all_to_all | solution.py:57
  27.2 5.1 %copy-start.1 = (bf16[8,4,2,64,128]{4,3,1,0,2:T(8,128)(2,1)}, bf16[8,4,2,64,128]{4,3,1,0,2:T(8,128)(2,1)S(1)}, u32[]{:S(2)}) copy-start(bf16[8,4,2,64,128]{4,3,1,0,2:T(8,128)(2,1)S(1)} %all-to-all-done.3) | copy-start | bytes 3145732
  27.2 11.6 %all-to-all-start.1 = ((s32[16,1,1,4]{3,2,1,0:T(1,128)}), s32[16,1,1,4]{3,2,1,0:T(1,128)}, u32[]{:S(2)}, u32[]{:S(2)}) async-start(s32[16,1,1,4]{3,2,1,0:T(1,128)} %copy.43), calls=%async_computation.1 | async-start | bytes 16384 | tf_op jit(solution)/shard_map/all_to_all | solution.py:73
  89.6 10.3 %all-to-all-start.2 = ((s32[1,1,16,4]{3,1,0,2:T(1,128)}), s32[1,1,16,4]{3,1,0,2:T(1,128)S(1)}, u32[]{:S(2)}, u32[]{:S(2)}) async-start(s32[1,1,16,4]{3,1,0,2:T(1,128)} %bitcast.31), calls=%async_computation.2 | async-start | bytes 16384 | tf_op jit(solution)/shard_map/all_to_all | solution.py:72
